TPU v7x, 32 devices: a whole 2x2x4 slice. The times are simulated.
32 devices in a mesh: gx: 2 (over x), gy: 4 (over y, core), gz: 4 (over z).
Axes of the slice: x: 2, y: 2, z: 4, core: 2. Of those that a mesh axis runs over, the one named last changes fastest.
Arguments:
- displacement: float32 [3, 16, 32, 512], P(None, 'gx', 'gz', 'gy'), may hold values from -0.1 to 0.1
- velocity: float32 [3, 16, 32, 512], P(None, 'gx', 'gz', 'gy'), may hold values from -0.4 to 0.4
- body_force: float32 [3, 16, 32, 512], P(None, 'gx', 'gz', 'gy'), may hold values from -4 to 4
- broken: int32 [12, 16, 32, 512], P(None, 'gx', 'gz', 'gy'), may hold values from 0 to 1073741823
Outputs:
- new_displacement: float32 [3, 16, 32, 512], P(None, 'gx', 'gz', 'gy')
- new_velocity: float32 [3, 16, 32, 512], P(None, 'gx', 'gz', 'gy')
- new_acceleration: float32 [3, 16, 32, 512], P(None, 'gx', 'gz', 'gy')
- strain_energy: float32 [], replicated
All inputs are finite; a program needn't handle non-finite values.
Results may differ from a plain program's by a relative error of at most 0.0003.
Values sent between devices are 32-bit elements; how exact they have to be, the bound alone decides.
A program may use at most 128 MiB of HBM per device.

v0:
```python
import functools
import math

import jax
import jax.numpy as jnp
from jax import lax
from jax.experimental import pallas as pl
from jax.experimental.pallas import tpu as pltpu
from jax.sharding import PartitionSpec as P

TIME_STEP = 0.05
MICRO_MODULUS = 4.0
BITS_PER_WORD = 30
W = 3
REACH = range(-W, W + 1)
BONDS = tuple(
    (p, q, r) for p in REACH for q in REACH for r in REACH if (p, q, r) != (0, 0, 0)
)
INDEX = {bond: k for k, bond in enumerate(BONDS)}
WORD_COUNT = -(-len(BONDS) // BITS_PER_WORD)


def extended(block, axis, dim):
    count = lax.axis_size(axis)
    forward = [(i, (i + 1) % count) for i in range(count)]
    backward = [(t, s) for s, t in forward]
    low = lax.ppermute(
        lax.slice_in_dim(block, block.shape[dim] - W, None, axis=dim), axis, forward
    )
    high = lax.ppermute(lax.slice_in_dim(block, 0, W, axis=dim), axis, backward)
    return low, high


def depth_bits(shape, depth_start, depth_total):
    depth = lax.broadcasted_iota(jnp.int32, shape, 0) + depth_start
    words = [jnp.zeros(shape, jnp.int32) for _ in range(WORD_COUNT)]
    for q in REACH:
        if q == 0:
            continue
        outside = (depth + q < 0) | (depth + q >= depth_total)
        for w in range(WORD_COUNT):
            bits = 0
            for (p, q2, r), k in INDEX.items():
                if q2 == q and k // BITS_PER_WORD == w:
                    bits |= 1 << (k % BITS_PER_WORD)
            if bits:
                words[w] = words[w] | jnp.where(outside, bits, 0)
    return words


def store_masks(broken_ref, mask_ref, outside_ref, depth_start, depth_total):
    rows = broken_ref.shape[1]
    for w, word in enumerate(depth_bits(broken_ref.shape[2:], depth_start, depth_total)):
        outside_ref[w] = word

    def body(x, carry):
        for w in range(WORD_COUNT):
            word = broken_ref[w, x] | outside_ref[w]
            for k in range(w * BITS_PER_WORD, min(len(BONDS), (w + 1) * BITS_PER_WORD)):
                p, q, r = BONDS[k]
                weight = MICRO_MODULUS * math.exp(-(p * p + q * q + r * r) / 9.0)
                bit = word & (1 << (k % BITS_PER_WORD))
                mask_ref[k, x] = jnp.where(bit == 0, jnp.float32(weight), jnp.float32(0.0))
        return carry

    lax.fori_loop(0, rows, body, 0)


def shifted_rows(a, b, lane, e_ref, c, x):
    width = a.shape[1]
    depth = a.shape[0]
    for r in REACH:
        if r == 0:
            tile = a
        elif r > 0:
            tile = pltpu.roll(jnp.where(lane < r, b, a), width - r, 1)
        else:
            tile = pltpu.roll(jnp.where(lane >= width + r, b, a), -r, 1)
        if c == 2 and r != 0:
            tile = tile + float(r)
        e_ref[r + W, c, x, 0:depth] = tile


def bond_rows(x, steps, e_ref, mask_ref, depth, with_energy):
    center = [e_ref[W, c, x + W, W : W + depth] for c in range(3)]
    force = [jnp.zeros_like(center[0]) for _ in range(3)]
    energy = jnp.zeros_like(center[0])
    for p in steps:
        center_x = center[0] - float(p)
        for q in REACH:
            center_z = center[1] - float(q)
            for r in REACH:
                if (p, q, r) == (0, 0, 0):
                    continue
                k = INDEX[(p, q, r)]
                rest = math.sqrt(p * p + q * q + r * r)
                nb = [
                    e_ref[r + W, c, x + (W + p), W + q : W + q + depth] for c in range(3)
                ]
                bx = nb[0] - center_x
                bz = nb[1] - center_z
                by = nb[2] - center[2]
                square = bx * bx + bz * bz + by * by
                h = jnp.float32(1.0 / rest) - lax.rsqrt(square)
                g = mask_ref[k, x] * h
                force[0] = force[0] + g * bx
                force[1] = force[1] + g * bz
                force[2] = force[2] + g * by
                if with_energy:
                    energy = energy + (g * jnp.float32(0.25 * rest)) * (h * square)
    return force, energy


def pass_kernel(
    depth_total, with_energy, a_ref, b_ref, broken_ref, force_ref, energy_ref,
    e_ref, mask_ref, outside_ref,
):
    rows, depth = broken_ref.shape[1], broken_ref.shape[2]
    width = a_ref.shape[3]
    depth_start = lax.axis_index("gz") * depth
    store_masks(broken_ref, mask_ref, outside_ref, depth_start, depth_total)
    lane = lax.broadcasted_iota(jnp.int32, a_ref.shape[2:], 1)

    def fill(x, carry):
        for c in range(3):
            shifted_rows(a_ref[c, x], b_ref[c, x], lane, e_ref, c, x)
        return carry

    lax.fori_loop(0, rows + 2 * W, fill, 0)
    energy_ref[...] = jnp.zeros_like(energy_ref)

    def body(x, carry):
        force, energy = bond_rows(x, REACH, e_ref, mask_ref, depth, with_energy)
        for c in range(3):
            force_ref[c, x] = force[c]
        if with_energy:
            energy_ref[...] += energy
        return carry

    lax.fori_loop(0, rows, body, 0)


def bond_sum(field, broken, with_energy):
    _, rows, depth, width = field.shape
    depth_total = depth * lax.axis_size("gz")
    low, high = extended(field, "gx", 1)
    field = jnp.concatenate([low, field, high], axis=1)
    low, high = extended(field, "gz", 2)
    field = jnp.concatenate([low, field, high], axis=2)
    low, high = extended(field, "gy", 3)
    sides = jnp.concatenate(
        [high, jnp.zeros(field.shape[:3] + (width - 2 * W,), field.dtype), low], axis=3
    )
    padded = -(-(depth + 2 * W) // 8) * 8
    return pl.pallas_call(
        functools.partial(pass_kernel, depth_total, with_energy),
        out_shape=(
            jax.ShapeDtypeStruct((3, rows, depth, width), jnp.float32),
            jax.ShapeDtypeStruct((depth, width), jnp.float32),
        ),
        in_specs=[pl.BlockSpec(memory_space=pltpu.VMEM)] * 3,
        out_specs=(pl.BlockSpec(memory_space=pltpu.VMEM),) * 2,
        scratch_shapes=[
            pltpu.VMEM((2 * W + 1, 3, rows + 2 * W, padded, width), jnp.float32),
            pltpu.VMEM((len(BONDS), rows, depth, width), jnp.float32),
            pltpu.VMEM((WORD_COUNT, depth, width), jnp.int32),
        ],
        compiler_params=pltpu.CompilerParams(vmem_limit_bytes=48 * 1024 * 1024),
    )(field, sides, broken)


def per_device(displacement, velocity, body_force, broken):
    rows, width = displacement.shape[1], displacement.shape[3]
    first_force, unused = bond_sum(displacement, broken, False)
    first_acceleration = first_force + body_force
    new_displacement = (
        displacement + TIME_STEP * velocity + 0.5 * TIME_STEP * TIME_STEP * first_acceleration
    )
    second_force, local_energy = bond_sum(new_displacement, broken, True)
    new_acceleration = second_force + body_force
    new_velocity = velocity + 0.5 * TIME_STEP * (first_acceleration + new_acceleration)
    total_energy = lax.psum(jnp.sum(local_energy), ("gx", "gy", "gz"))
    area = rows * lax.axis_size("gx") * width * lax.axis_size("gy")
    strain_energy = total_energy / jnp.float32(area)
    return (new_displacement, new_velocity, new_acceleration, strain_energy)


def solution(mesh):
    spec = P(None, "gx", "gz", "gy")
    return jax.shard_map(
        per_device,
        mesh=mesh,
        in_specs=(spec,) * 4,
        out_specs=(spec, spec, spec, P()),
        check_vma=False,
    )
```

profile of v0, /device:TPU:0, one launch (start us, length us, event | category | flops | bytes accessed | tf_op | source)
XLA Modules:
  0.0 114.8 jit_solution(3981506966979253219)
XLA Ops:
  0.6 0.8 fusion.5
  1.5 3.0 %collective-permute-start = (f32[3,3,8,128]{3,2,1,0:T(8,128)S(1)}, f32[3,3,8,128]{3,2,1,0:T(8,128)S(1)}, u32[]{:S(2)}, u32[]{:S(2)}) collective-permute-start(f32[3,3,8,128]{3,2,1,0:T(8,128)S(1)} %get-tuple-element.25), channel_id=1, source_target_pairs={{0,16},{16,0},{1,17},{17,1},{2,18},{18,2},{3,19},{19,3},{4,20},{20... | collective-permute-start | bytes 110600 | tf_op jit(solution)/shard_map/ppermute | solution.py:27
  4.4 0.1 collective-permute-start.1
  4.5 1.9 %collective-permute-done = f32[3,3,8,128]{3,2,1,0:T(8,128)S(1)} collective-permute-done((f32[3,3,8,128]{3,2,1,0:T(8,128)S(1)}, f32[3,3,8,128]{3,2,1,0:T(8,128)S(1)}, u32[]{:S(2)}, u32[]{:S(2)}) %collective-permute-start) | collective-permute-done | bytes 36896 | tf_op jit(solution)/shard_map/ppermute | solution.py:27
  6.4 2.0 %collective-permute-done.1 = f32[3,3,8,128]{3,2,1,0:T(8,128)S(1)} collective-permute-done((f32[3,3,8,128]{3,2,1,0:T(8,128)S(1)}, f32[3,3,8,128]{3,2,1,0:T(8,128)S(1)}, u32[]{:S(2)}, u32[]{:S(2)}) %collective-permute-start.1) | collective-permute-done | bytes 36896 | tf_op jit(solution)/shard_map/ppermute | solution.py:30
  8.4 1.6 %collective-permute-start.2 = (f32[3,14,3,128]{3,2,1,0:T(4,128)S(1)}, f32[3,14,3,128]{3,2,1,0:T(4,128)S(1)}, u32[]{:S(2)}, u32[]{:S(2)}) collective-permute-start(f32[3,14,3,128]{3,2,1,0:T(4,128)S(1)} %get-tuple-element.20), channel_id=1, source_target_pairs={{0,1},{1,2},{2,3},{3,0},{4,5},{5,6},{6,7},{7,4},{8,9},{9,10},{10,1... | collective-permute-start | bytes 193544 | tf_op jit(solution)/shard_map/ppermute | solution.py:27
  10.1 2.2 %collective-permute-start.3 = (f32[3,14,3,128]{3,2,1,0:T(4,128)S(1)}, f32[3,14,3,128]{3,2,1,0:T(4,128)S(1)}, u32[]{:S(2)}, u32[]{:S(2)}) collective-permute-start(f32[3,14,3,128]{3,2,1,0:T(4,128)S(1)} %get-tuple-element.21), channel_id=1, source_target_pairs={{1,0},{2,1},{3,2},{0,3},{5,4},{6,5},{7,6},{4,7},{9,8},{10,9},{11,1... | collective-permute-start | bytes 193544 | tf_op jit(solution)/shard_map/ppermute | solution.py:30
  12.3 3.0 %collective-permute-done.2 = f32[3,14,3,128]{3,2,1,0:T(4,128)S(1)} collective-permute-done((f32[3,14,3,128]{3,2,1,0:T(4,128)S(1)}, f32[3,14,3,128]{3,2,1,0:T(4,128)S(1)}, u32[]{:S(2)}, u32[]{:S(2)}) %collective-permute-start.2) | collective-permute-done | bytes 64544 | tf_op jit(solution)/shard_map/ppermute | solution.py:27
  15.3 0.2 collective-permute-done.3
  15.5 0.2 fusion.1
  15.8 0.5 collective-permute-start.5
  16.3 0.1 pad.12.clone
  16.4 6.9 %collective-permute-done.4 = f32[3,14,14,3]{3,2,1,0:T(8,128)S(1)} collective-permute-done((f32[3,14,14,3]{3,2,1,0:T(8,128)S(1)}, f32[3,14,14,3]{3,2,1,0:T(8,128)S(1)}, u32[]{:S(2)}, u32[]{:S(2)}) %collective-permute-start.4) | collective-permute-done | bytes 7088 | tf_op jit(solution)/shard_map/ppermute | solution.py:30
  23.2 3.0 %collective-permute-done.5 = f32[3,14,14,3]{3,2,1,0:T(8,128)S(1)} collective-permute-done((f32[3,14,14,3]{3,2,1,0:T(8,128)S(1)}, f32[3,14,14,3]{3,2,1,0:T(8,128)S(1)}, u32[]{:S(2)}, u32[]{:S(2)}) %collective-permute-start.5) | collective-permute-done | bytes 7088 | tf_op jit(solution)/shard_map/ppermute | solution.py:27
  26.2 0.2 pad_maximum_fusion.1.b_ref
  26.4 11.8 %shard_map.75 = (f32[3,8,8,128]{3,2,1,0:T(8,128)S(1)}, f32[8,128]{1,0:T(8,128)}) custom-call(f32[3,14,14,128]{3,2,1,0:T(8,128)S(1)} %pad_maximum_fusion.a_ref, f32[3,14,14,128]{3,2,1,0:T(8,128)S(1)} %pad_maximum_fusion.1.b_ref, s32[12,8,8,128]{3,2,1,0:T(8,128)S(1)} %copy-done), custom_call_target="tpu_custom_call" | custom-call | tf_op jit(solution)/shard_map/pallas_call | solution.py:155
  38.2 0.6 collective-permute-start.6
  38.8 1.5 %collective-permute-start.7 = (f32[3,3,8,128]{3,2,1,0:T(8,128)S(1)}, f32[3,3,8,128]{3,2,1,0:T(8,128)S(1)}, u32[]{:S(2)}, u32[]{:S(2)}) collective-permute-start(f32[3,3,8,128]{3,2,1,0:T(8,128)S(1)} %get-tuple-element.23), channel_id=1, source_target_pairs={{16,0},{0,16},{17,1},{1,17},{18,2},{2,18},{19,3},{3,19},{20,4},{4,... | collective-permute-start | bytes 110600 | tf_op jit(solution)/shard_map/ppermute | solution.py:30
  40.3 1.9 %collective-permute-done.6 = f32[3,3,8,128]{3,2,1,0:T(8,128)S(1)} collective-permute-done((f32[3,3,8,128]{3,2,1,0:T(8,128)S(1)}, f32[3,3,8,128]{3,2,1,0:T(8,128)S(1)}, u32[]{:S(2)}, u32[]{:S(2)}) %collective-permute-start.6) | collective-permute-done | bytes 36896 | tf_op jit(solution)/shard_map/ppermute | solution.py:27
  42.3 0.5 collective-permute-done.7
  42.9 1.1 collective-permute-start.8
  43.9 2.8 %collective-permute-start.9 = (f32[3,14,3,128]{3,2,1,0:T(4,128)S(1)}, f32[3,14,3,128]{3,2,1,0:T(4,128)S(1)}, u32[]{:S(2)}, u32[]{:S(2)}) collective-permute-start(f32[3,14,3,128]{3,2,1,0:T(4,128)S(1)} %get-tuple-element.19), channel_id=1, source_target_pairs={{1,0},{2,1},{3,2},{0,3},{5,4},{6,5},{7,6},{4,7},{9,8},{10,9},{11,1... | collective-permute-start | bytes 193544 | tf_op jit(solution)/shard_map/ppermute | solution.py:30
  46.7 2.6 %collective-permute-done.8 = f32[3,14,3,128]{3,2,1,0:T(4,128)S(1)} collective-permute-done((f32[3,14,3,128]{3,2,1,0:T(4,128)S(1)}, f32[3,14,3,128]{3,2,1,0:T(4,128)S(1)}, u32[]{:S(2)}, u32[]{:S(2)}) %collective-permute-start.8) | collective-permute-done | bytes 64544 | tf_op jit(solution)/shard_map/ppermute | solution.py:27
  49.4 0.2 fusion
  49.7 0.5 collective-permute-start.11
  50.2 7.9 %collective-permute-done.10 = f32[3,14,14,3]{3,2,1,0:T(8,128)S(1)} collective-permute-done((f32[3,14,14,3]{3,2,1,0:T(8,128)S(1)}, f32[3,14,14,3]{3,2,1,0:T(8,128)S(1)}, u32[]{:S(2)}, u32[]{:S(2)}) %collective-permute-start.10) | collective-permute-done | bytes 7088 | tf_op jit(solution)/shard_map/ppermute | solution.py:30
  58.1 1.0 collective-permute-done.11
  59.1 0.2 pad_maximum_fusion.3.b_ref
  59.2 12.4 %shard_map.76 = (f32[3,8,8,128]{3,2,1,0:T(8,128)S(1)}, f32[8,128]{1,0:T(8,128)S(1)}) custom-call(f32[3,14,14,128]{3,2,1,0:T(8,128)S(1)} %pad_maximum_fusion.2.a_ref, f32[3,14,14,128]{3,2,1,0:T(8,128)S(1)} %pad_maximum_fusion.3.b_ref, s32[12,8,8,128]{3,2,1,0:T(8,128)S(1)} %copy-done), custom_call_target="tpu_custom_call" | custom-call | tf_op jit(solution)/shard_map/pallas_call | solution.py:155
  71.6 0.6 reduce_sum.9
  72.2 40.1 %psum.7 = f32[]{:T(128)} all-reduce(f32[]{:T(128)} %reduce_sum.9), channel_id=1, replica_groups=mesh['gx'=2,'gy'=4,'gz'=4] {'gx','gy','gz'}, use_global_device_ids=true, to_apply=%region_1.0 | all-reduce | flops 1 | bytes 8 | tf_op jit(solution)/shard_map/psum | solution.py:182
  113.0 0.7 multiply_add_fusion
  (24 shorter events, 0.5 us)
Async XLA Ops:
  0.6 5.8 %copy-start.2 = (f32[3,8,8,128]{3,2,1,0:T(8,128)S(1)}, f32[3,8,8,128]{3,2,1,0:T(8,128)}, u32[]{:S(2)}) copy-start(f32[3,8,8,128]{3,2,1,0:T(8,128)} %param.4) | copy-start | bytes 294916
  1.5 4.9 %collective-permute-start = (f32[3,3,8,128]{3,2,1,0:T(8,128)S(1)}, f32[3,3,8,128]{3,2,1,0:T(8,128)S(1)}, u32[]{:S(2)}, u32[]{:S(2)}) collective-permute-start(f32[3,3,8,128]{3,2,1,0:T(8,128)S(1)} %get-tuple-element.25), channel_id=1, source_target_pairs={{0,16},{16,0},{1,17},{17,1},{2,18},{18,2},{3,19},{19,3},{4,20},{20... | collective-permute-start | bytes 110600 | tf_op jit(solution)/shard_map/ppermute | solution.py:27
  4.4 4.0 %collective-permute-start.1 = (f32[3,3,8,128]{3,2,1,0:T(8,128)S(1)}, f32[3,3,8,128]{3,2,1,0:T(8,128)S(1)}, u32[]{:S(2)}, u32[]{:S(2)}) collective-permute-start(f32[3,3,8,128]{3,2,1,0:T(8,128)S(1)} %get-tuple-element.24), channel_id=1, source_target_pairs={{16,0},{0,16},{17,1},{1,17},{18,2},{2,18},{19,3},{3,19},{20,4},{4,... | collective-permute-start | bytes 110600 | tf_op jit(solution)/shard_map/ppermute | solution.py:30
  8.4 6.9 %collective-permute-start.2 = (f32[3,14,3,128]{3,2,1,0:T(4,128)S(1)}, f32[3,14,3,128]{3,2,1,0:T(4,128)S(1)}, u32[]{:S(2)}, u32[]{:S(2)}) collective-permute-start(f32[3,14,3,128]{3,2,1,0:T(4,128)S(1)} %get-tuple-element.20), channel_id=1, source_target_pairs={{0,1},{1,2},{2,3},{3,0},{4,5},{5,6},{6,7},{7,4},{8,9},{9,10},{10,1... | collective-permute-start | bytes 193544 | tf_op jit(solution)/shard_map/ppermute | solution.py:27
  10.1 5.4 %collective-permute-start.3 = (f32[3,14,3,128]{3,2,1,0:T(4,128)S(1)}, f32[3,14,3,128]{3,2,1,0:T(4,128)S(1)}, u32[]{:S(2)}, u32[]{:S(2)}) collective-permute-start(f32[3,14,3,128]{3,2,1,0:T(4,128)S(1)} %get-tuple-element.21), channel_id=1, source_target_pairs={{1,0},{2,1},{3,2},{0,3},{5,4},{6,5},{7,6},{4,7},{9,8},{10,9},{11,1... | collective-permute-start | bytes 193544 | tf_op jit(solution)/shard_map/ppermute | solution.py:30
  15.7 7.5 %collective-permute-start.4 = (f32[3,14,14,3]{3,2,1,0:T(8,128)S(1)}, f32[3,14,14,3]{3,2,1,0:T(8,128)S(1)}, u32[]{:S(2)}, u32[]{:S(2)}) collective-permute-start(f32[3,14,14,3]{3,2,1,0:T(8,128)S(1)} %get-tuple-element.16), channel_id=1, source_target_pairs={{4,0},{8,4},{12,8},{0,12},{5,1},{9,5},{13,9},{1,13},{6,2},{10,6},{... | collective-permute-start | bytes 21176 | tf_op jit(solution)/shard_map/ppermute | solution.py:30
  15.8 10.4 %collective-permute-start.5 = (f32[3,14,14,3]{3,2,1,0:T(8,128)S(1)}, f32[3,14,14,3]{3,2,1,0:T(8,128)S(1)}, u32[]{:S(2)}, u32[]{:S(2)}) collective-permute-start(f32[3,14,14,3]{3,2,1,0:T(8,128)S(1)} %get-tuple-element.17), channel_id=1, source_target_pairs={{0,4},{4,8},{8,12},{12,0},{1,5},{5,9},{9,13},{13,1},{2,6},{6,10},{... | collective-permute-start | bytes 21176 | tf_op jit(solution)/shard_map/ppermute | solution.py:27
  16.4 10.0 %copy-start = (s32[12,8,8,128]{3,2,1,0:T(8,128)S(1)}, s32[12,8,8,128]{3,2,1,0:T(8,128)}, u32[]{:S(2)}) copy-start(s32[12,8,8,128]{3,2,1,0:T(8,128)} %broken_ref.3) | copy-start | bytes 1179652
  26.4 11.8 %copy-start.3 = (f32[3,8,8,128]{3,2,1,0:T(8,128)S(1)}, f32[3,8,8,128]{3,2,1,0:T(8,128)}, u32[]{:S(2)}) copy-start(f32[3,8,8,128]{3,2,1,0:T(8,128)} %param.5) | copy-start | bytes 294916
  26.4 11.8 %copy-start.4 = (f32[3,8,8,128]{3,2,1,0:T(8,128)S(1)}, f32[3,8,8,128]{3,2,1,0:T(8,128)}, u32[]{:S(2)}) copy-start(f32[3,8,8,128]{3,2,1,0:T(8,128)} %param.6) | copy-start | bytes 294916
  38.2 11.1 %copy-start.1 = (f32[3,8,8,128]{3,2,1,0:T(8,128)}, f32[3,8,8,128]{3,2,1,0:T(8,128)S(1)}, u32[]{:S(2)}) copy-start(f32[3,8,8,128]{3,2,1,0:T(8,128)S(1)} %get-tuple-element.12) | copy-start | bytes 294916
  38.2 4.0 %collective-permute-start.6 = (f32[3,3,8,128]{3,2,1,0:T(8,128)S(1)}, f32[3,3,8,128]{3,2,1,0:T(8,128)S(1)}, u32[]{:S(2)}, u32[]{:S(2)}) collective-permute-start(f32[3,3,8,128]{3,2,1,0:T(8,128)S(1)} %get-tuple-element.22), channel_id=1, source_target_pairs={{0,16},{16,0},{1,17},{17,1},{2,18},{18,2},{3,19},{19,3},{4,20},{20... | collective-permute-start | bytes 110600 | tf_op jit(solution)/shard_map/ppermute | solution.py:27
  38.8 4.0 %collective-permute-start.7 = (f32[3,3,8,128]{3,2,1,0:T(8,128)S(1)}, f32[3,3,8,128]{3,2,1,0:T(8,128)S(1)}, u32[]{:S(2)}, u32[]{:S(2)}) collective-permute-start(f32[3,3,8,128]{3,2,1,0:T(8,128)S(1)} %get-tuple-element.23), channel_id=1, source_target_pairs={{16,0},{0,16},{17,1},{1,17},{18,2},{2,18},{19,3},{3,19},{20,4},{4,... | collective-permute-start | bytes 110600 | tf_op jit(solution)/shard_map/ppermute | solution.py:30
  42.9 6.4 %collective-permute-start.8 = (f32[3,14,3,128]{3,2,1,0:T(4,128)S(1)}, f32[3,14,3,128]{3,2,1,0:T(4,128)S(1)}, u32[]{:S(2)}, u32[]{:S(2)}) collective-permute-start(f32[3,14,3,128]{3,2,1,0:T(4,128)S(1)} %get-tuple-element.18), channel_id=1, source_target_pairs={{0,1},{1,2},{2,3},{3,0},{4,5},{5,6},{6,7},{7,4},{8,9},{9,10},{10,1... | collective-permute-start | bytes 193544 | tf_op jit(solution)/shard_map/ppermute | solution.py:27
  43.9 5.4 %collective-permute-start.9 = (f32[3,14,3,128]{3,2,1,0:T(4,128)S(1)}, f32[3,14,3,128]{3,2,1,0:T(4,128)S(1)}, u32[]{:S(2)}, u32[]{:S(2)}) collective-permute-start(f32[3,14,3,128]{3,2,1,0:T(4,128)S(1)} %get-tuple-element.19), channel_id=1, source_target_pairs={{1,0},{2,1},{3,2},{0,3},{5,4},{6,5},{7,6},{4,7},{9,8},{10,9},{11,1... | collective-permute-start | bytes 193544 | tf_op jit(solution)/shard_map/ppermute | solution.py:30
  49.6 8.5 %collective-permute-start.10 = (f32[3,14,14,3]{3,2,1,0:T(8,128)S(1)}, f32[3,14,14,3]{3,2,1,0:T(8,128)S(1)}, u32[]{:S(2)}, u32[]{:S(2)}) collective-permute-start(f32[3,14,14,3]{3,2,1,0:T(8,128)S(1)} %get-tuple-element.14), channel_id=1, source_target_pairs={{4,0},{8,4},{12,8},{0,12},{5,1},{9,5},{13,9},{1,13},{6,2},{10,6},{... | collective-permute-start | bytes 21176 | tf_op jit(solution)/shard_map/ppermute | solution.py:30
  49.7 9.4 %collective-permute-start.11 = (f32[3,14,14,3]{3,2,1,0:T(8,128)S(1)}, f32[3,14,14,3]{3,2,1,0:T(8,128)S(1)}, u32[]{:S(2)}, u32[]{:S(2)}) collective-permute-start(f32[3,14,14,3]{3,2,1,0:T(8,128)S(1)} %get-tuple-element.15), channel_id=1, source_target_pairs={{0,4},{4,8},{8,12},{12,0},{1,5},{5,9},{9,13},{13,1},{2,6},{6,10},{... | collective-permute-start | bytes 21176 | tf_op jit(solution)/shard_map/ppermute | solution.py:27
where the time goes:
time: 115 us
  blocking collectives  40.1 us (35%)
  waiting for transfers between devices  30.9 us (27%)
  Pallas kernels  24.2 us (21%)
  starting transfers between devices  14 us (12%)
  between operations  2.56 us (2%)
  other arithmetic  1.8 us (2%)
  local copies, waits for them, and re-layouts  1.36 us (1%)
    psum x1, blocking collectives, per_device(): total_energy = lax.psum(jnp.sum(local_energy), ('gx', 'gy', 'gz'))  40.1 us
    pallas_call x2, Pallas kernels, bond_sum(): pl.pallas_call(functools.partial(pass_kernel, depth_total, with_energy),...  24.2 us
    ppermute x6, waiting for transfers between devices, extended(): high = lax.ppermute(lax.slice_in_dim(block, 0, W, axis=dim), axis, backward)  17.6 us
    ppermute x6, waiting for transfers between devices, extended(): lax.ppermute(lax.slice_in_dim(block, block.shape[dim] - W, None, axis=dim...  13.3 us
    ppermute x6, starting transfers between devices, extended(): lax.ppermute(lax.slice_in_dim(block, block.shape[dim] - W, None, axis=dim...  7.28 us
    ppermute x6, starting transfers between devices, extended(): high = lax.ppermute(lax.slice_in_dim(block, 0, W, axis=dim), axis, backward)  6.71 us
  transfers between devices with their start and end apart: 12, of which 12 were waited for; matrix products, arithmetic and copies ran while one was open for 0% of the time, Pallas kernels for 0%

commit v1 on v0

--- a/solution.py
+++ b/solution.py
@@ -169,6 +169,64 @@
     )(field, sides, broken)
 
 
+AXES = ("gx", "gy", "gz")
+
+
+def sum_kernel(counts, tile_ref, total_ref, *scratch):
+    slots, (send_sem, recv_sem) = scratch[: len(AXES)], scratch[len(AXES) :]
+    barrier = pltpu.get_barrier_semaphore()
+    peers = 0
+    for axis, count in zip(AXES, counts):
+        me = lax.axis_index(axis)
+        for d in range(1, count):
+            pl.semaphore_signal(
+                barrier,
+                inc=1,
+                device_id={axis: lax.rem(me + d, count)},
+                device_id_type=pl.DeviceIdType.MESH,
+            )
+            peers += 1
+    pl.semaphore_wait(barrier, peers)
+    at = 0
+    value = tile_ref[...]
+    for slot, axis, count in zip(slots, AXES, counts):
+        me = lax.axis_index(axis)
+        slot[me] = value
+        copies = []
+        for d in range(1, count):
+            copy = pltpu.make_async_remote_copy(
+                src_ref=slot.at[me],
+                dst_ref=slot.at[me],
+                send_sem=send_sem.at[at],
+                recv_sem=recv_sem.at[at],
+                device_id={axis: lax.rem(me + d, count)},
+                device_id_type=pl.DeviceIdType.MESH,
+            )
+            copy.start()
+            copies.append(copy)
+            at += 1
+        for copy in copies:
+            copy.wait()
+        value = slot[0]
+        for i in range(1, count):
+            value = value + slot[i]
+    total_ref[...] = value
+
+
+def mesh_sum(tile):
+    counts = tuple(lax.axis_size(axis) for axis in AXES)
+    peers = sum(counts) - len(counts)
+    return pl.pallas_call(
+        functools.partial(sum_kernel, counts),
+        out_shape=jax.ShapeDtypeStruct(tile.shape, tile.dtype),
+        in_specs=[pl.BlockSpec(memory_space=pltpu.VMEM)],
+        out_specs=pl.BlockSpec(memory_space=pltpu.VMEM),
+        scratch_shapes=[pltpu.VMEM((count,) + tile.shape, tile.dtype) for count in counts]
+        + [pltpu.SemaphoreType.DMA((peers,)), pltpu.SemaphoreType.DMA((peers,))],
+        compiler_params=pltpu.CompilerParams(collective_id=0, has_side_effects=True),
+    )(tile)
+
+
 def per_device(displacement, velocity, body_force, broken):
     rows, width = displacement.shape[1], displacement.shape[3]
     first_force, unused = bond_sum(displacement, broken, False)
@@ -179,7 +237,7 @@
     second_force, local_energy = bond_sum(new_displacement, broken, True)
     new_acceleration = second_force + body_force
     new_velocity = velocity + 0.5 * TIME_STEP * (first_acceleration + new_acceleration)
-    total_energy = lax.psum(jnp.sum(local_energy), ("gx", "gy", "gz"))
+    total_energy = jnp.sum(mesh_sum(local_energy))
     area = rows * lax.axis_size("gx") * width * lax.axis_size("gy")
     strain_energy = total_energy / jnp.float32(area)
     return (new_displacement, new_velocity, new_acceleration, strain_energy)

time: 115 us -> 89.7 us (0.78)
  blocking collectives: 40.1 us -> 0 us
  Pallas kernels: 24.2 us -> 37.6 us
    psum x1 -> x0, blocking collectives: 40.1 us -> none  [per_device(): total_energy = lax.psum(jnp.sum(local_energy), ('gx', 'gy', 'gz'))]
    pallas_call x0 -> x1, Pallas kernels: none -> 13.4 us  [mesh_sum(): pl.pallas_call(functools.partial(sum_kernel, counts), out_shape=jax.Shape...]
where the time goes in v1:
time: 89.7 us; the launch traced here: 89.4 us
  Pallas kernels  37.6 us (42%)
  waiting for transfers between devices  30.9 us (34%)
  starting transfers between devices  14 us (16%)
  between operations  2.57 us (3%)
  other arithmetic  2.47 us (3%)
  local copies, waits for them, and re-layouts  1.94 us (2%)
    pallas_call x2, Pallas kernels, bond_sum(): pl.pallas_call(functools.partial(pass_kernel, depth_total, with_energy),...  24.2 us
    ppermute x6, waiting for transfers between devices, extended(): high = lax.ppermute(lax.slice_in_dim(block, 0, W, axis=dim), axis, backward)  17.6 us
    pallas_call x1, Pallas kernels, mesh_sum(): pl.pallas_call(functools.partial(sum_kernel, counts), out_shape=jax.Shape...  13.4 us
    ppermute x6, waiting for transfers between devices, extended(): lax.ppermute(lax.slice_in_dim(block, block.shape[dim] - W, None, axis=dim...  13.3 us
    ppermute x6, starting transfers between devices, extended(): lax.ppermute(lax.slice_in_dim(block, block.shape[dim] - W, None, axis=dim...  7.28 us
    ppermute x6, starting transfers between devices, extended(): high = lax.ppermute(lax.slice_in_dim(block, 0, W, axis=dim), axis, backward)  6.71 us
  transfers between devices with their start and end apart: 12, of which 12 were waited for; matrix products, arithmetic and copies ran while one was open for 0% of the time, Pallas kernels for 0%

profile of v1, /device:TPU:0, one launch (start us, length us, event | category | flops | bytes accessed | tf_op | source)
XLA Modules:
  0.0 89.4 jit_solution(7271818565743848953)
XLA Ops:
  0.6 0.8 fusion.5
  1.5 3.0 %collective-permute-start = (f32[3,3,8,128]{3,2,1,0:T(8,128)S(1)}, f32[3,3,8,128]{3,2,1,0:T(8,128)S(1)}, u32[]{:S(2)}, u32[]{:S(2)}) collective-permute-start(f32[3,3,8,128]{3,2,1,0:T(8,128)S(1)} %get-tuple-element.25), channel_id=1, source_target_pairs={{0,16},{16,0},{1,17},{17,1},{2,18},{18,2},{3,19},{19,3},{4,20},{20... | collective-permute-start | bytes 110600 | tf_op jit(solution)/shard_map/ppermute | solution.py:27
  4.5 1.9 %collective-permute-done = f32[3,3,8,128]{3,2,1,0:T(8,128)S(1)} collective-permute-done((f32[3,3,8,128]{3,2,1,0:T(8,128)S(1)}, f32[3,3,8,128]{3,2,1,0:T(8,128)S(1)}, u32[]{:S(2)}, u32[]{:S(2)}) %collective-permute-start) | collective-permute-done | bytes 36896 | tf_op jit(solution)/shard_map/ppermute | solution.py:27
  6.4 2.0 %collective-permute-done.1 = f32[3,3,8,128]{3,2,1,0:T(8,128)S(1)} collective-permute-done((f32[3,3,8,128]{3,2,1,0:T(8,128)S(1)}, f32[3,3,8,128]{3,2,1,0:T(8,128)S(1)}, u32[]{:S(2)}, u32[]{:S(2)}) %collective-permute-start.1) | collective-permute-done | bytes 36896 | tf_op jit(solution)/shard_map/ppermute | solution.py:30
  8.4 1.6 %collective-permute-start.2 = (f32[3,14,3,128]{3,2,1,0:T(4,128)S(1)}, f32[3,14,3,128]{3,2,1,0:T(4,128)S(1)}, u32[]{:S(2)}, u32[]{:S(2)}) collective-permute-start(f32[3,14,3,128]{3,2,1,0:T(4,128)S(1)} %get-tuple-element.20), channel_id=1, source_target_pairs={{0,1},{1,2},{2,3},{3,0},{4,5},{5,6},{6,7},{7,4},{8,9},{9,10},{10,1... | collective-permute-start | bytes 193544 | tf_op jit(solution)/shard_map/ppermute | solution.py:27
  10.1 2.2 %collective-permute-start.3 = (f32[3,14,3,128]{3,2,1,0:T(4,128)S(1)}, f32[3,14,3,128]{3,2,1,0:T(4,128)S(1)}, u32[]{:S(2)}, u32[]{:S(2)}) collective-permute-start(f32[3,14,3,128]{3,2,1,0:T(4,128)S(1)} %get-tuple-element.21), channel_id=1, source_target_pairs={{1,0},{2,1},{3,2},{0,3},{5,4},{6,5},{7,6},{4,7},{9,8},{10,9},{11,1... | collective-permute-start | bytes 193544 | tf_op jit(solution)/shard_map/ppermute | solution.py:30
  12.3 3.0 %collective-permute-done.2 = f32[3,14,3,128]{3,2,1,0:T(4,128)S(1)} collective-permute-done((f32[3,14,3,128]{3,2,1,0:T(4,128)S(1)}, f32[3,14,3,128]{3,2,1,0:T(4,128)S(1)}, u32[]{:S(2)}, u32[]{:S(2)}) %collective-permute-start.2) | collective-permute-done | bytes 64544 | tf_op jit(solution)/shard_map/ppermute | solution.py:27
  15.3 0.2 collective-permute-done.3
  15.5 0.2 fusion.1
  15.8 0.5 collective-permute-start.5
  16.3 0.1 pad.12.clone
  16.4 6.9 %collective-permute-done.4 = f32[3,14,14,3]{3,2,1,0:T(8,128)S(1)} collective-permute-done((f32[3,14,14,3]{3,2,1,0:T(8,128)S(1)}, f32[3,14,14,3]{3,2,1,0:T(8,128)S(1)}, u32[]{:S(2)}, u32[]{:S(2)}) %collective-permute-start.4) | collective-permute-done | bytes 7088 | tf_op jit(solution)/shard_map/ppermute | solution.py:30
  23.2 3.0 %collective-permute-done.5 = f32[3,14,14,3]{3,2,1,0:T(8,128)S(1)} collective-permute-done((f32[3,14,14,3]{3,2,1,0:T(8,128)S(1)}, f32[3,14,14,3]{3,2,1,0:T(8,128)S(1)}, u32[]{:S(2)}, u32[]{:S(2)}) %collective-permute-start.5) | collective-permute-done | bytes 7088 | tf_op jit(solution)/shard_map/ppermute | solution.py:27
  26.2 0.2 pad_maximum_fusion.1.b_ref
  26.4 11.8 %shard_map.75 = (f32[3,8,8,128]{3,2,1,0:T(8,128)S(1)}, f32[8,128]{1,0:T(8,128)}) custom-call(f32[3,14,14,128]{3,2,1,0:T(8,128)S(1)} %pad_maximum_fusion.a_ref, f32[3,14,14,128]{3,2,1,0:T(8,128)S(1)} %pad_maximum_fusion.1.b_ref, s32[12,8,8,128]{3,2,1,0:T(8,128)S(1)} %copy-done), custom_call_target="tpu_custom_call" | custom-call | tf_op jit(solution)/shard_map/pallas_call | solution.py:155
  38.2 0.6 collective-permute-start.6
  38.8 1.5 %collective-permute-start.7 = (f32[3,3,8,128]{3,2,1,0:T(8,128)S(1)}, f32[3,3,8,128]{3,2,1,0:T(8,128)S(1)}, u32[]{:S(2)}, u32[]{:S(2)}) collective-permute-start(f32[3,3,8,128]{3,2,1,0:T(8,128)S(1)} %get-tuple-element.23), channel_id=1, source_target_pairs={{16,0},{0,16},{17,1},{1,17},{18,2},{2,18},{19,3},{3,19},{20,4},{4,... | collective-permute-start | bytes 110600 | tf_op jit(solution)/shard_map/ppermute | solution.py:30
  40.3 1.9 %collective-permute-done.6 = f32[3,3,8,128]{3,2,1,0:T(8,128)S(1)} collective-permute-done((f32[3,3,8,128]{3,2,1,0:T(8,128)S(1)}, f32[3,3,8,128]{3,2,1,0:T(8,128)S(1)}, u32[]{:S(2)}, u32[]{:S(2)}) %collective-permute-start.6) | collective-permute-done | bytes 36896 | tf_op jit(solution)/shard_map/ppermute | solution.py:27
  42.3 0.5 collective-permute-done.7
  42.8 1.1 %collective-permute-start.8 = (f32[3,14,3,128]{3,2,1,0:T(4,128)S(1)}, f32[3,14,3,128]{3,2,1,0:T(4,128)S(1)}, u32[]{:S(2)}, u32[]{:S(2)}) collective-permute-start(f32[3,14,3,128]{3,2,1,0:T(4,128)S(1)} %get-tuple-element.18), channel_id=1, source_target_pairs={{0,1},{1,2},{2,3},{3,0},{4,5},{5,6},{6,7},{7,4},{8,9},{9,10},{10,1... | collective-permute-start | bytes 193544 | tf_op jit(solution)/shard_map/ppermute | solution.py:27
  43.9 2.8 %collective-permute-start.9 = (f32[3,14,3,128]{3,2,1,0:T(4,128)S(1)}, f32[3,14,3,128]{3,2,1,0:T(4,128)S(1)}, u32[]{:S(2)}, u32[]{:S(2)}) collective-permute-start(f32[3,14,3,128]{3,2,1,0:T(4,128)S(1)} %get-tuple-element.19), channel_id=1, source_target_pairs={{1,0},{2,1},{3,2},{0,3},{5,4},{6,5},{7,6},{4,7},{9,8},{10,9},{11,1... | collective-permute-start | bytes 193544 | tf_op jit(solution)/shard_map/ppermute | solution.py:30
  46.7 2.6 %collective-permute-done.8 = f32[3,14,3,128]{3,2,1,0:T(4,128)S(1)} collective-permute-done((f32[3,14,3,128]{3,2,1,0:T(4,128)S(1)}, f32[3,14,3,128]{3,2,1,0:T(4,128)S(1)}, u32[]{:S(2)}, u32[]{:S(2)}) %collective-permute-start.8) | collective-permute-done | bytes 64544 | tf_op jit(solution)/shard_map/ppermute | solution.py:27
  49.4 0.2 fusion
  49.7 0.5 collective-permute-start.11
  50.1 7.9 %collective-permute-done.10 = f32[3,14,14,3]{3,2,1,0:T(8,128)S(1)} collective-permute-done((f32[3,14,14,3]{3,2,1,0:T(8,128)S(1)}, f32[3,14,14,3]{3,2,1,0:T(8,128)S(1)}, u32[]{:S(2)}, u32[]{:S(2)}) %collective-permute-start.10) | collective-permute-done | bytes 7088 | tf_op jit(solution)/shard_map/ppermute | solution.py:30
  58.1 1.0 %collective-permute-done.11 = f32[3,14,14,3]{3,2,1,0:T(8,128)S(1)} collective-permute-done((f32[3,14,14,3]{3,2,1,0:T(8,128)S(1)}, f32[3,14,14,3]{3,2,1,0:T(8,128)S(1)}, u32[]{:S(2)}, u32[]{:S(2)}) %collective-permute-start.11) | collective-permute-done | bytes 7088 | tf_op jit(solution)/shard_map/ppermute | solution.py:27
  59.1 0.2 pad_maximum_fusion.3.b_ref
  59.2 12.4 %shard_map.76 = (f32[3,8,8,128]{3,2,1,0:T(8,128)S(1)}, f32[8,128]{1,0:T(8,128)S(1)}) custom-call(f32[3,14,14,128]{3,2,1,0:T(8,128)S(1)} %pad_maximum_fusion.2.a_ref, f32[3,14,14,128]{3,2,1,0:T(8,128)S(1)} %pad_maximum_fusion.3.b_ref, s32[12,8,8,128]{3,2,1,0:T(8,128)S(1)} %copy-done), custom_call_target="tpu_custom_call" | custom-call | tf_op jit(solution)/shard_map/pallas_call | solution.py:155
  71.6 0.6 copy-done.1
  72.2 13.4 %shard_map.77 = f32[8,128]{1,0:T(8,128)} custom-call(f32[8,128]{1,0:T(8,128)} %copy-done.1), custom_call_target="tpu_custom_call" | custom-call | tf_op jit(solution)/shard_map/pallas_call | solution.py:219
  85.7 1.3 %reduce_sum.9 = f32[]{:T(128)} reduce(f32[8,128]{1,0:T(8,128)} %shard_map.77, f32[]{:T(128)} %constant.1.clone.1), dimensions={0,1}, to_apply=%region_0.0 | reduce | flops 1023 | bytes 4104 | tf_op jit(solution)/shard_map/reduce_sum | solution.py:240
  87.0 0.7 multiply_add_fusion
  (26 shorter events, 0.5 us)
Async XLA Ops:
  0.6 5.8 %copy-start.3 = (f32[3,8,8,128]{3,2,1,0:T(8,128)S(1)}, f32[3,8,8,128]{3,2,1,0:T(8,128)}, u32[]{:S(2)}) copy-start(f32[3,8,8,128]{3,2,1,0:T(8,128)} %param.4) | copy-start | bytes 294916
  1.5 4.9 %collective-permute-start = (f32[3,3,8,128]{3,2,1,0:T(8,128)S(1)}, f32[3,3,8,128]{3,2,1,0:T(8,128)S(1)}, u32[]{:S(2)}, u32[]{:S(2)}) collective-permute-start(f32[3,3,8,128]{3,2,1,0:T(8,128)S(1)} %get-tuple-element.25), channel_id=1, source_target_pairs={{0,16},{16,0},{1,17},{17,1},{2,18},{18,2},{3,19},{19,3},{4,20},{20... | collective-permute-start | bytes 110600 | tf_op jit(solution)/shard_map/ppermute | solution.py:27
  4.4 4.0 %collective-permute-start.1 = (f32[3,3,8,128]{3,2,1,0:T(8,128)S(1)}, f32[3,3,8,128]{3,2,1,0:T(8,128)S(1)}, u32[]{:S(2)}, u32[]{:S(2)}) collective-permute-start(f32[3,3,8,128]{3,2,1,0:T(8,128)S(1)} %get-tuple-element.24), channel_id=1, source_target_pairs={{16,0},{0,16},{17,1},{1,17},{18,2},{2,18},{19,3},{3,19},{20,4},{4,... | collective-permute-start | bytes 110600 | tf_op jit(solution)/shard_map/ppermute | solution.py:30
  8.4 6.9 %collective-permute-start.2 = (f32[3,14,3,128]{3,2,1,0:T(4,128)S(1)}, f32[3,14,3,128]{3,2,1,0:T(4,128)S(1)}, u32[]{:S(2)}, u32[]{:S(2)}) collective-permute-start(f32[3,14,3,128]{3,2,1,0:T(4,128)S(1)} %get-tuple-element.20), channel_id=1, source_target_pairs={{0,1},{1,2},{2,3},{3,0},{4,5},{5,6},{6,7},{7,4},{8,9},{9,10},{10,1... | collective-permute-start | bytes 193544 | tf_op jit(solution)/shard_map/ppermute | solution.py:27
  10.1 5.4 %collective-permute-start.3 = (f32[3,14,3,128]{3,2,1,0:T(4,128)S(1)}, f32[3,14,3,128]{3,2,1,0:T(4,128)S(1)}, u32[]{:S(2)}, u32[]{:S(2)}) collective-permute-start(f32[3,14,3,128]{3,2,1,0:T(4,128)S(1)} %get-tuple-element.21), channel_id=1, source_target_pairs={{1,0},{2,1},{3,2},{0,3},{5,4},{6,5},{7,6},{4,7},{9,8},{10,9},{11,1... | collective-permute-start | bytes 193544 | tf_op jit(solution)/shard_map/ppermute | solution.py:30
  15.7 7.5 %collective-permute-start.4 = (f32[3,14,14,3]{3,2,1,0:T(8,128)S(1)}, f32[3,14,14,3]{3,2,1,0:T(8,128)S(1)}, u32[]{:S(2)}, u32[]{:S(2)}) collective-permute-start(f32[3,14,14,3]{3,2,1,0:T(8,128)S(1)} %get-tuple-element.16), channel_id=1, source_target_pairs={{4,0},{8,4},{12,8},{0,12},{5,1},{9,5},{13,9},{1,13},{6,2},{10,6},{... | collective-permute-start | bytes 21176 | tf_op jit(solution)/shard_map/ppermute | solution.py:30
  15.8 10.4 %collective-permute-start.5 = (f32[3,14,14,3]{3,2,1,0:T(8,128)S(1)}, f32[3,14,14,3]{3,2,1,0:T(8,128)S(1)}, u32[]{:S(2)}, u32[]{:S(2)}) collective-permute-start(f32[3,14,14,3]{3,2,1,0:T(8,128)S(1)} %get-tuple-element.17), channel_id=1, source_target_pairs={{0,4},{4,8},{8,12},{12,0},{1,5},{5,9},{9,13},{13,1},{2,6},{6,10},{... | collective-permute-start | bytes 21176 | tf_op jit(solution)/shard_map/ppermute | solution.py:27
  16.4 10.0 %copy-start = (s32[12,8,8,128]{3,2,1,0:T(8,128)S(1)}, s32[12,8,8,128]{3,2,1,0:T(8,128)}, u32[]{:S(2)}) copy-start(s32[12,8,8,128]{3,2,1,0:T(8,128)} %broken_ref.3) | copy-start | bytes 1179652
  26.4 11.8 %copy-start.4 = (f32[3,8,8,128]{3,2,1,0:T(8,128)S(1)}, f32[3,8,8,128]{3,2,1,0:T(8,128)}, u32[]{:S(2)}) copy-start(f32[3,8,8,128]{3,2,1,0:T(8,128)} %param.5) | copy-start | bytes 294916
  26.4 11.8 %copy-start.5 = (f32[3,8,8,128]{3,2,1,0:T(8,128)S(1)}, f32[3,8,8,128]{3,2,1,0:T(8,128)}, u32[]{:S(2)}) copy-start(f32[3,8,8,128]{3,2,1,0:T(8,128)} %param.6) | copy-start | bytes 294916
  38.2 11.1 %copy-start.2 = (f32[3,8,8,128]{3,2,1,0:T(8,128)}, f32[3,8,8,128]{3,2,1,0:T(8,128)S(1)}, u32[]{:S(2)}) copy-start(f32[3,8,8,128]{3,2,1,0:T(8,128)S(1)} %get-tuple-element.12) | copy-start | bytes 294916
  38.2 4.0 %collective-permute-start.6 = (f32[3,3,8,128]{3,2,1,0:T(8,128)S(1)}, f32[3,3,8,128]{3,2,1,0:T(8,128)S(1)}, u32[]{:S(2)}, u32[]{:S(2)}) collective-permute-start(f32[3,3,8,128]{3,2,1,0:T(8,128)S(1)} %get-tuple-element.22), channel_id=1, source_target_pairs={{0,16},{16,0},{1,17},{17,1},{2,18},{18,2},{3,19},{19,3},{4,20},{20... | collective-permute-start | bytes 110600 | tf_op jit(solution)/shard_map/ppermute | solution.py:27
  38.8 4.0 %collective-permute-start.7 = (f32[3,3,8,128]{3,2,1,0:T(8,128)S(1)}, f32[3,3,8,128]{3,2,1,0:T(8,128)S(1)}, u32[]{:S(2)}, u32[]{:S(2)}) collective-permute-start(f32[3,3,8,128]{3,2,1,0:T(8,128)S(1)} %get-tuple-element.23), channel_id=1, source_target_pairs={{16,0},{0,16},{17,1},{1,17},{18,2},{2,18},{19,3},{3,19},{20,4},{4,... | collective-permute-start | bytes 110600 | tf_op jit(solution)/shard_map/ppermute | solution.py:30
  42.8 6.4 %collective-permute-start.8 = (f32[3,14,3,128]{3,2,1,0:T(4,128)S(1)}, f32[3,14,3,128]{3,2,1,0:T(4,128)S(1)}, u32[]{:S(2)}, u32[]{:S(2)}) collective-permute-start(f32[3,14,3,128]{3,2,1,0:T(4,128)S(1)} %get-tuple-element.18), channel_id=1, source_target_pairs={{0,1},{1,2},{2,3},{3,0},{4,5},{5,6},{6,7},{7,4},{8,9},{9,10},{10,1... | collective-permute-start | bytes 193544 | tf_op jit(solution)/shard_map/ppermute | solution.py:27
  43.9 5.4 %collective-permute-start.9 = (f32[3,14,3,128]{3,2,1,0:T(4,128)S(1)}, f32[3,14,3,128]{3,2,1,0:T(4,128)S(1)}, u32[]{:S(2)}, u32[]{:S(2)}) collective-permute-start(f32[3,14,3,128]{3,2,1,0:T(4,128)S(1)} %get-tuple-element.19), channel_id=1, source_target_pairs={{1,0},{2,1},{3,2},{0,3},{5,4},{6,5},{7,6},{4,7},{9,8},{10,9},{11,1... | collective-permute-start | bytes 193544 | tf_op jit(solution)/shard_map/ppermute | solution.py:30
  49.6 8.5 %collective-permute-start.10 = (f32[3,14,14,3]{3,2,1,0:T(8,128)S(1)}, f32[3,14,14,3]{3,2,1,0:T(8,128)S(1)}, u32[]{:S(2)}, u32[]{:S(2)}) collective-permute-start(f32[3,14,14,3]{3,2,1,0:T(8,128)S(1)} %get-tuple-element.14), channel_id=1, source_target_pairs={{4,0},{8,4},{12,8},{0,12},{5,1},{9,5},{13,9},{1,13},{6,2},{10,6},{... | collective-permute-start | bytes 21176 | tf_op jit(solution)/shard_map/ppermute | solution.py:30
  49.7 9.4 %collective-permute-start.11 = (f32[3,14,14,3]{3,2,1,0:T(8,128)S(1)}, f32[3,14,14,3]{3,2,1,0:T(8,128)S(1)}, u32[]{:S(2)}, u32[]{:S(2)}) collective-permute-start(f32[3,14,14,3]{3,2,1,0:T(8,128)S(1)} %get-tuple-element.15), channel_id=1, source_target_pairs={{0,4},{4,8},{8,12},{12,0},{1,5},{5,9},{9,13},{13,1},{2,6},{6,10},{... | collective-permute-start | bytes 21176 | tf_op jit(solution)/shard_map/ppermute | solution.py:27
  71.6 0.6 copy-start.1
